TPU v7x, 32 devices: a whole 2x2x4 slice. The times are simulated.
32 devices in a mesh: gx: 8 (over y, x, core), wa: 4 (over z).
Axes of the slice: x: 2, y: 2, z: 4, core: 2. Of those that a mesh axis runs over, the one named last changes fastest.
Arguments:
- warm_field: float32 [64, 2, 128, 2048], P('wa', None, 'gx'), may hold values from -1.8 to 1.8
- warm_adjoint: float32 [64, 2, 128, 2048], P('wa', None, 'gx'), may hold values from -1.8 to 1.8
- permittivity: float32 [128, 2048], P('gx'), may hold values from 1 to 12
- design_mask: int32 [128, 2048], P('gx'), may hold values 0 or 1
- source_row: int32 [64], P('wa'), may hold values from 0 to 127
- monitor_row: int32 [64], P('wa'), may hold values from 0 to 127
- wavenumber: float32 [64], P('wa'), may hold values from 0.02 to 0.08
- bloch_phase: float32 [64], P('wa'), may hold values from -3.140625 to 3.140625
- source_profile: float32 [64, 2, 2048], P('wa'), may hold values from -24 to 24
- monitor_profile: float32 [64, 2, 2048], P('wa'), may hold values from -4 to 4
Outputs:
- forward_field: float32 [64, 2, 128, 2048], P('wa', None, 'gx')
- adjoint_field: float32 [64, 2, 128, 2048], P('wa', None, 'gx')
- gradient: float32 [128, 2048], P('gx')
All inputs are finite; a program needn't handle non-finite values. No bound on the sum of `design_mask` on one device may be relied on, other than what follows from the above.
Results may differ from a plain program's by a relative error of at most 0.0003.
Values sent between devices are 32-bit elements; how exact they have to be, the bound alone decides.
A program may use at most 128 MiB of HBM per device.

v0:
```python
import functools

import jax
import jax.numpy as jnp
from jax import lax
from jax.experimental import pallas as pl
from jax.experimental.pallas import tpu as pltpu
from jax.sharding import PartitionSpec as P

floor_share = 0.5
REACH = 3
TILE = 8
LANES = 128
QUARTERS = 4
SUMS = 16
VMEM_LIMIT = 50000 * 1024


def col(tile):
    return slice(tile * LANES, (tile + 1) * LANES)


def sideways(load, tiles):
    tile = load(0)
    lane = lax.broadcasted_iota(jnp.int32, tile.shape, 1)
    at_right, at_left = lane == LANES - 1, lane == 0
    after, before = pltpu.roll(tile, LANES - 1, 1), pltpu.roll(tile, 1, 1)
    carried = jnp.zeros_like(tile)
    for ct in range(tiles):
        if ct + 1 < tiles:
            ahead = load(ct + 1)
            next_after, next_before = pltpu.roll(ahead, LANES - 1, 1), pltpu.roll(ahead, 1, 1)
        else:
            ahead, next_after, next_before = None, jnp.zeros_like(tile), None
        near = jnp.where(at_right, next_after, after) + jnp.where(at_left, carried, before)
        yield near
        carried, tile, after, before = before, ahead, next_after, next_before


def updown(tile):
    total = tile.shape[0]
    return pltpu.roll(tile, total - 1, 0) + pltpu.roll(tile, 1, 0)


def fold(cells):
    acc = cells[:TILE]
    for start in range(TILE, cells.shape[0], TILE):
        acc = acc + cells[start : start + TILE]
    return acc


def pair_products(a, b):
    return fold(a[0] * b[0] + a[1] * b[1]), fold(a[0] * b[1] - a[1] * b[0])


def times(a, b):
    return a[0] * b[0] - a[1] * b[1], a[0] * b[1] + a[1] * b[0]


def scalars_of(total, with_overlap):
    q = [total[:, i : i + 1] for i in range(SUMS)]
    res_norm, rv_re, rv_im, image_sq, wr_re, wr_im, wv_re, wv_im, twice_sq = q[:9]
    half = floor_share * res_norm
    bounded = jnp.maximum(rv_re * rv_re + rv_im * rv_im, half * half)
    step_re = res_norm * rv_re / bounded
    step_im = -res_norm * rv_im / bounded
    step_sq = step_re * step_re + step_im * step_im
    ts_re = rv_re - step_re * image_sq - (step_re * wr_re + step_im * wr_im) + step_sq * wv_re
    ts_im = -rv_im - step_im * image_sq - (step_re * wr_im - step_im * wr_re) + step_sq * wv_im
    tt_sum = image_sq - 2.0 * (step_re * wv_re + step_im * wv_im) + step_sq * twice_sq
    omega_re = ts_re / tt_sum
    omega_im = ts_im / tt_sum
    both_re, both_im = times((step_re, step_im), (omega_re, omega_im))
    found = [step_re + omega_re, step_im + omega_im, -both_re, -both_im]
    if with_overlap:
        mx_re, mx_im, mz_re, mz_im, my_re, my_im = q[9:15]
        for_z = times(found[0:2], (mz_re, mz_im))
        for_y = times(found[2:4], (my_re, my_im))
        found.append(mx_re + for_z[0] + for_y[0])
        found.append(mx_im + for_z[1] + for_y[1])
    return found


def step_kernel(
    count, depth,
    turns, wave_k, src_row, mon_row, eps_hbm, field_hbm, adjoint_hbm, mask_hbm, src_hbm, mon_hbm,
    fwd, adj, grad,
    ext, zed, yed, send, recv, res, img, diag, inverse, eps, eps_send, eps_recv, src, mon, mask,
    parts, mine, got, coef, gpart, ggot, gtotal, gspread,
    load_sem, side_sem, halo_sems, eps_sems, sum_sems, grad_sems,
):
    waves, _, rows, width = field_hbm.shape
    total = rows + TILE
    tiles = width // LANES
    quarter = width // QUARTERS
    whole = rows * count
    me = lax.axis_index("gx")
    level = lax.axis_index("wa")
    before, after = lax.rem(me - 1 + count, count), lax.rem(me + 1, count)
    at_first, at_last = me == 0, me == count - 1

    fields = (field_hbm, adjoint_hbm)

    def load(field, wave):
        return pltpu.make_async_copy(
            fields[field].at[wave], ext.at[field, wave, :, pl.ds(0, rows)],
            load_sem.at[field, wave],
        )

    sides = [
        pltpu.make_async_copy(eps_hbm, eps.at[pl.ds(0, rows)], side_sem.at[0]),
        pltpu.make_async_copy(src_hbm, src, side_sem.at[1]),
        pltpu.make_async_copy(mon_hbm, mon, side_sem.at[2]),
        pltpu.make_async_copy(mask_hbm, mask, side_sem.at[3]),
    ]
    sides[0].start()
    for wave in range(waves):
        load(0, wave).start()
    for copy in sides[1:]:
        copy.start()
    for wave in range(waves):
        load(1, wave).start()

    barrier = pltpu.get_barrier_semaphore()
    for axis, size, own in (("gx", count, me), ("wa", depth, level)):
        for hop in range(1, size):
            pl.semaphore_signal(
                barrier, inc=1, device_id={axis: lax.rem(own + hop, size)},
                device_id_type=pl.DeviceIdType.MESH,
            )

    sides[0].wait()
    for way, low in ((0, 0), (1, rows - REACH)):
        for part in range(QUARTERS):
            span = slice(part * quarter, (part + 1) * quarter)
            eps_send[way, part * 4 : part * 4 + REACH] = eps[low : low + REACH, span]

    def neighbour(way):
        return {"gx": before if way == 0 else after}

    def eps_move(way):
        return pltpu.make_async_remote_copy(
            src_ref=eps_send.at[way], dst_ref=eps_recv.at[way],
            send_sem=eps_sems.at[0, way], recv_sem=eps_sems.at[1, way],
            device_id=neighbour(way), device_id_type=pl.DeviceIdType.MESH,
        )

    def halo_move(field, way, wave):
        return pltpu.make_async_remote_copy(
            src_ref=send.at[field, way, wave], dst_ref=recv.at[field, way, wave],
            send_sem=halo_sems.at[0, field, way, wave],
            recv_sem=halo_sems.at[1, field, way, wave],
            device_id=neighbour(way), device_id_type=pl.DeviceIdType.MESH,
        )

    def pack(field, wave):
        for way, low in ((0, 0), (1, rows - REACH)):
            for c in range(2):
                for part in range(QUARTERS):
                    span = slice(part * quarter, (part + 1) * quarter)
                    at = part * 2 * REACH + c * REACH
                    send[field, way, wave, at : at + REACH] = ext[
                        field, wave, c, low : low + REACH, span
                    ]

    pl.semaphore_wait(barrier, count - 1 + depth - 1)
    for way in range(2):
        eps_move(way).start()

    def first_sends(wave, carry):
        load(0, wave).wait()
        pack(0, wave)
        for way in range(2):
            halo_move(0, way, wave).start()
        return carry

    lax.fori_loop(0, waves, first_sends, 0)
    for copy in sides[1:]:
        copy.wait()

    def adjoint_packs(wave, carry):
        load(1, wave).wait()
        pack(1, wave)
        return carry

    lax.fori_loop(0, waves, adjoint_packs, 0)

    for way, at in ((0, rows), (1, total - REACH)):
        eps_move(way).wait_recv()
        for part in range(QUARTERS):
            span = slice(part * quarter, (part + 1) * quarter)
            eps[at : at + REACH, span] = eps_recv[way, part * 4 : part * 4 + REACH]
    eps[rows + REACH : total - REACH] = jnp.ones((TILE - 2 * REACH, width), jnp.float32)

    row_of = lax.broadcasted_iota(jnp.int32, (total, LANES), 0)

    def spot_of(row):
        away = row - me * rows
        away = jnp.where(away < 0, away + whole, away)
        spot = jnp.where(
            away < rows + REACH, away,
            jnp.where(away >= whole - REACH, away - whole + total, -1),
        )
        return spot

    def turn_of(spot, wave, sign):
        cosine, sine = turns[0, wave], sign * turns[1, wave]
        above = (spot >= rows) & (spot < rows + REACH) & at_last
        below = (spot >= rows + REACH) & at_first
        turn_c = jnp.where(above | below, cosine, 1.0)
        turn_s = jnp.where(above, sine, jnp.where(below, -sine, 0.0))
        return turn_c, turn_s

    def unpack(field, wave, sign):
        cosine, sine = turns[0, wave], sign * turns[1, wave]
        for way, at in ((0, rows), (1, total - REACH)):
            edge = at_last if way == 0 else at_first
            turn_c = jnp.where(edge, cosine, 1.0)
            turn_s = jnp.where(edge, sine if way == 0 else -sine, 0.0)
            for part in range(QUARTERS):
                span = slice(part * quarter, (part + 1) * quarter)
                base = part * 2 * REACH
                got_re = recv[field, way, wave, base : base + REACH]
                got_im = recv[field, way, wave, base + REACH : base + 2 * REACH]
                ext[field, wave, 0, at : at + REACH, span] = turn_c * got_re - turn_s * got_im
                ext[field, wave, 1, at : at + REACH, span] = turn_s * got_re + turn_c * got_im

    def images(field, wave, spot, side_row, with_overlap):
        squared_k = wave_k[wave]
        for ct in range(tiles):
            d = 4.0 - squared_k * eps[:, col(ct)]
            diag[:, col(ct)] = d
            inverse[:, col(ct)] = 1.0 / d
        here = row_of == spot
        nears = [
            sideways(lambda ct, c=c: ext[field, wave, c, :, col(ct)], tiles) for c in range(2)
        ]
        for ct in range(tiles):
            rows_in = side_row(ct)
            for c in range(2):
                near = next(nears[c])
                x = ext[field, wave, c, :, col(ct)]
                r = (near + updown(x)) - diag[:, col(ct)] * x
                r = jnp.where(here, r + rows_in[c], r)
                res[c, :, col(ct)] = r
                zed[wave, c, :, col(ct)] = r * inverse[:, col(ct)]
        nears = [sideways(lambda ct, c=c: zed[wave, c, :, col(ct)], tiles) for c in range(2)]
        for ct in range(tiles):
            for c in range(2):
                near = next(nears[c])
                v = res[c, :, col(ct)] - (near + updown(zed[wave, c, :, col(ct)]))
                img[c, :, col(ct)] = v[:rows]
                yed[wave, c, :, col(ct)] = v * inverse[:, col(ct)]
        nears = [
            sideways(lambda ct, c=c: yed[wave, c, 0:rows, col(ct)], tiles) for c in range(2)
        ]
        sums = None
        for ct in range(tiles):
            r, v, w = [], [], []
            for c in range(2):
                near = next(nears[c])
                r.append(res[c, 0:rows, col(ct)])
                v.append(img[c, :, col(ct)])
                w.append(v[c] - (near + updown(yed[wave, c, :, col(ct)])[:rows]))
            found = [
                fold(r[0] * r[0] + r[1] * r[1]), *pair_products(r, v),
                fold(v[0] * v[0] + v[1] * v[1]), *pair_products(w, r), *pair_products(w, v),
                fold(w[0] * w[0] + w[1] * w[1]),
            ]
            sums = found if sums is None else [a + b for a, b in zip(sums, found)]
        for i, value in enumerate(sums):
            parts[i, pl.ds(wave, 1)] = jnp.sum(value, axis=0, keepdims=True)
        if with_overlap:
            away = mon_row[wave] - me * rows
            inside = jnp.where((away >= 0) & (away < rows), 1.0, 0.0)
            place = jnp.clip(away, 0, rows - 1)
            held = (
                lambda c: ext[field, wave, c, pl.ds(place, 1)],
                lambda c: zed[wave, c, pl.ds(place, 1)],
                lambda c: yed[wave, c, pl.ds(place, 1)],
            )
            for i, get in enumerate(held):
                sum_re = sum_im = None
                lines = [get(c) for c in range(2)]
                for ct in range(tiles):
                    m = [mon[wave, c : c + 1, col(ct)] for c in range(2)]
                    f = [line[:, col(ct)] for line in lines]
                    new_re = m[0] * f[0] + m[1] * f[1]
                    new_im = m[0] * f[1] - m[1] * f[0]
                    sum_re = new_re if sum_re is None else sum_re + new_re
                    sum_im = new_im if sum_im is None else sum_im + new_im
                parts[9 + 2 * i, pl.ds(wave, 1)] = inside * sum_re
                parts[10 + 2 * i, pl.ds(wave, 1)] = inside * sum_im

    def profile_row(profile, wave, turn, over):
        turn_c, turn_s = turn

        def row(ct):
            p = [profile[wave, c : c + 1, col(ct)] for c in range(2)]
            if over is not None:
                p_re, p_im = times(over, p)
                p = [p_re, -p_im]
            return turn_c * p[0] - turn_s * p[1], turn_s * p[0] + turn_c * p[1]

        return row

    def sum_over_gx(field):
        used = 15 if field == 0 else 9
        lane = lax.broadcasted_iota(jnp.int32, (waves, LANES), 1)
        packed = jnp.zeros((waves, LANES), jnp.float32)
        for i in range(used):
            packed = jnp.where(lane == i, jnp.sum(parts[i], axis=1, keepdims=True), packed)
        mine[field] = packed

        def move(hop, place):
            return pltpu.make_async_remote_copy(
                src_ref=mine.at[field], dst_ref=got.at[field, place],
                send_sem=sum_sems.at[0, field, hop], recv_sem=sum_sems.at[1, field, hop],
                device_id={"gx": lax.rem(me + hop, count)},
                device_id_type=pl.DeviceIdType.MESH,
            )

        for hop in range(1, count):
            move(hop, me).start()
        got[field, me] = packed
        for hop in range(1, count):
            move(hop, lax.rem(me - hop + count, count)).wait_recv()
        summed = got[field, 0]
        for place in range(1, count):
            summed = summed + got[field, place]
        for i, value in enumerate(scalars_of(summed, field == 0)):
            coef[field, i] = jnp.broadcast_to(value, (waves, LANES))
        for hop in range(1, count):
            move(hop, me).wait_send()

    def factors(field, wave, *slots):
        return [coef[field, i, pl.ds(wave, 1)] for i in slots]

    def result(field, wave, b, g, span):
        x = [ext[field, wave, c, 0:rows, span] for c in range(2)]
        z = [zed[wave, c, 0:rows, span] for c in range(2)]
        y = [yed[wave, c, 0:rows, span] for c in range(2)]
        bz, gy = times(b, z), times(g, y)
        return x[0] + bz[0] + gy[0], x[1] + bz[1] + gy[1]

    def forward_images(wave, carry):
        for way in range(2):
            halo_move(1, way, wave).start()
        for way in range(2):
            halo_move(0, way, wave).wait_recv()
        unpack(0, wave, 1.0)
        spot = spot_of(src_row[wave])
        images(0, wave, spot, profile_row(src, wave, turn_of(spot, wave, 1.0), None), True)
        return carry

    lax.fori_loop(0, waves, forward_images, 0)
    sum_over_gx(0)

    def adjoint_images(wave, carry):
        b, g, over = factors(0, wave, 0, 1), factors(0, wave, 2, 3), factors(0, wave, 4, 5)
        for ct in range(tiles):
            fwd[wave, 0, :, col(ct)], fwd[wave, 1, :, col(ct)] = result(0, wave, b, g, col(ct))
        for way in range(2):
            halo_move(1, way, wave).wait_recv()
        unpack(1, wave, -1.0)
        spot = spot_of(mon_row[wave])
        images(1, wave, spot, profile_row(mon, wave, turn_of(spot, wave, -1.0), over), False)
        return carry

    lax.fori_loop(0, waves, adjoint_images, 0)
    sum_over_gx(1)

    piece = width // depth

    def columns(place):
        return slice(place * piece, (place + 1) * piece)

    def scatter(hop, to, place):
        return pltpu.make_async_remote_copy(
            src_ref=gpart.at[to], dst_ref=ggot.at[place],
            send_sem=grad_sems.at[0, hop], recv_sem=grad_sems.at[1, hop],
            device_id={"wa": lax.rem(level + hop, depth)}, device_id_type=pl.DeviceIdType.MESH,
        )

    def gather(hop, place):
        return pltpu.make_async_remote_copy(
            src_ref=gtotal, dst_ref=gspread.at[place],
            send_sem=grad_sems.at[2, hop], recv_sem=grad_sems.at[3, hop],
            device_id={"wa": lax.rem(level + hop, depth)}, device_id_type=pl.DeviceIdType.MESH,
        )

    for place in range(depth):
        def finish(wave, terms):
            b, g = factors(1, wave, 0, 1), factors(1, wave, 2, 3)
            scale = 2.0 * wave_k[wave]
            fresh = []
            for i in range(piece // LANES):
                span = col(place * (piece // LANES) + i)
                out_re, out_im = result(1, wave, b, g, span)
                adj[wave, 0, :, span] = out_re
                adj[wave, 1, :, span] = out_im
                fresh.append(
                    terms[i] + scale * (out_re * fwd[wave, 0, :, span] - out_im * fwd[wave, 1, :, span])
                )
            return tuple(fresh)

        terms = lax.fori_loop(
            0, waves, finish,
            tuple(jnp.zeros((rows, LANES), jnp.float32) for _ in range(piece // LANES)),
        )
        for i, term in enumerate(terms):
            gpart[place, :, col(i)] = term
    for hop in range(1, depth):
        scatter(hop, lax.rem(level + hop, depth), level).start()
    ggot[level] = gpart[level]
    for hop in range(1, depth):
        from_place = lax.rem(level - hop + depth, depth)
        scatter(hop, from_place, from_place).wait_recv()
    summed = ggot[0]
    for place in range(1, depth):
        summed = summed + ggot[place]
    gtotal[...] = summed
    for hop in range(1, depth):
        gather(hop, level).start()
    gspread[level] = summed
    for hop in range(1, depth):
        gather(hop, lax.rem(level - hop + depth, depth)).wait_recv()
    for place in range(depth):
        grad[:, columns(place)] = mask[:, columns(place)].astype(jnp.float32) * gspread[place]
    for hop in range(1, depth):
        scatter(hop, lax.rem(level + hop, depth), level).wait_send()
        gather(hop, level).wait_send()
    for way in range(2):
        eps_move(way).wait_send()

    def drain(wave, carry):
        for field in range(2):
            for way in range(2):
                halo_move(field, way, wave).wait_send()
        return carry

    lax.fori_loop(0, waves, drain, 0)


def write_kernel(fwd_in, adj_in, grad_in, fwd, adj, grad, sems):
    waves = fwd_in.shape[0]
    copies = []
    for wave in range(waves):
        copies.append(pltpu.make_async_copy(fwd_in.at[wave], fwd.at[wave], sems.at[0, wave]))
        copies.append(pltpu.make_async_copy(adj_in.at[wave], adj.at[wave], sems.at[1, wave]))
    for copy in copies:
        copy.start()
    grad[...] = grad_in[...]
    for copy in copies:
        copy.wait()


def local(
    warm_field,
    warm_adjoint,
    permittivity,
    design_mask,
    source_row,
    monitor_row,
    wavenumber,
    bloch_phase,
    source_profile,
    monitor_profile,
):
    waves, _, rows, width = warm_field.shape
    total = rows + TILE
    count, depth = lax.axis_size("gx"), lax.axis_size("wa")
    turns = jnp.stack([jnp.cos(bloch_phase), jnp.sin(bloch_phase)])

    smem = pl.BlockSpec(memory_space=pltpu.SMEM)
    vmem = pl.BlockSpec(memory_space=pltpu.VMEM)
    anywhere = pl.BlockSpec(memory_space=pl.ANY)
    f32 = jnp.float32
    piece = (rows, width // depth)
    block = (2 * REACH * QUARTERS, width // QUARTERS)
    fwd, adj, grad = pl.pallas_call(
        functools.partial(step_kernel, count, depth),
        out_shape=(
            pltpu.VMEM(warm_field.shape, f32),
            pltpu.VMEM(warm_field.shape, f32),
            pltpu.VMEM((rows, width), f32),
        ),
        in_specs=[smem] * 4 + [anywhere] * 6,
        out_specs=(vmem, vmem, vmem),
        scratch_shapes=[
            pltpu.VMEM((2, waves, 2, total, width), f32),
            pltpu.VMEM((waves, 2, total, width), f32),
            pltpu.VMEM((waves, 2, total, width), f32),
            pltpu.VMEM((2, 2, waves, *block), f32),
            pltpu.VMEM((2, 2, waves, *block), f32),
            pltpu.VMEM((2, total, width), f32),
            pltpu.VMEM((2, rows, width), f32),
            pltpu.VMEM((total, width), f32),
            pltpu.VMEM((total, width), f32),
            pltpu.VMEM((total, width), f32),
            pltpu.VMEM((2, 4 * QUARTERS, width // QUARTERS), f32),
            pltpu.VMEM((2, 4 * QUARTERS, width // QUARTERS), f32),
            pltpu.VMEM(source_profile.shape, f32),
            pltpu.VMEM(monitor_profile.shape, f32),
            pltpu.VMEM((rows, width), jnp.int32),
            pltpu.VMEM((SUMS, waves, LANES), f32),
            pltpu.VMEM((2, waves, LANES), f32),
            pltpu.VMEM((2, count, waves, LANES), f32),
            pltpu.VMEM((2, 6, waves, LANES), f32),
            pltpu.VMEM((depth, *piece), f32),
            pltpu.VMEM((depth, *piece), f32),
            pltpu.VMEM(piece, f32),
            pltpu.VMEM((depth, *piece), f32),
            pltpu.SemaphoreType.DMA((2, waves)),
            pltpu.SemaphoreType.DMA((4,)),
            pltpu.SemaphoreType.DMA((2, 2, 2, waves)),
            pltpu.SemaphoreType.DMA((2, 2)),
            pltpu.SemaphoreType.DMA((2, 2, count)),
            pltpu.SemaphoreType.DMA((4, depth)),
        ],
        compiler_params=pltpu.CompilerParams(
            collective_id=0, has_side_effects=True, vmem_limit_bytes=VMEM_LIMIT
        ),
        name="step",
    )(
        turns, wavenumber, source_row, monitor_row, permittivity, warm_field, warm_adjoint,
        design_mask, source_profile, monitor_profile,
    )
    field_shape = jax.ShapeDtypeStruct(warm_field.shape, f32)
    return pl.pallas_call(
        write_kernel,
        out_shape=(field_shape, field_shape, jax.ShapeDtypeStruct((rows, width), f32)),
        in_specs=[vmem, vmem, vmem],
        out_specs=(anywhere, anywhere, vmem),
        scratch_shapes=[pltpu.SemaphoreType.DMA((2, waves))],
        compiler_params=pltpu.CompilerParams(vmem_limit_bytes=1024 * 1024),
        name="write_out",
    )(fwd, adj, grad)


def solution(mesh):
    placed = (
        P("wa", None, "gx", None),
        P("wa", None, "gx", None),
        P("gx", None),
        P("gx", None),
        P("wa"),
        P("wa"),
        P("wa"),
        P("wa"),
        P("wa", None, None),
        P("wa", None, None),
    )
    return jax.shard_map(
        local,
        mesh=mesh,
        in_specs=placed,
        out_specs=(P("wa", None, "gx", None), P("wa", None, "gx", None), P("gx", None)),
        check_vma=False,
    )
```

profile of v0, /device:TPU:0, one launch (start us, length us, event | category | flops | bytes accessed | tf_op | source)
XLA Modules:
  0.0 79.7 jit_solution(917634027100505058)
XLA Ops:
  0.6 0.7 cosine_bitcast_fusion
  1.3 0.6 pad_maximum_fusion.turns
  1.9 73.6 %step.1 = (f32[16,2,16,2048]{3,2,1,0:T(8,128)S(1)}, f32[16,2,16,2048]{3,2,1,0:T(8,128)S(1)}, f32[16,2048]{1,0:T(8,128)S(1)}) custom-call(f32[2,16]{1,0:T(2,128)} %pad_maximum_fusion.turns, f32[16]{0:T(128)} %wave_k.1, s32[16]{0:T(128)} %src_row.1, s32[16]{0:T(128)} %mon_row.1, f32[16,2048]{1,0:T(8,128)} %eps_hbm.1, f32[16,2,16,2048]{3,2,1,0:T(8,128)} %field_hbm.1, ...), custom_call_target="tpu_custom_call" | custom-call | tf_op jit(solution)/shard_map/step/pallas_call | solution.py:481
  75.5 4.2 %write_out.1 = (f32[16,2,16,2048]{3,2,1,0:T(8,128)}, f32[16,2,16,2048]{3,2,1,0:T(8,128)}, f32[16,2048]{1,0:T(8,128)}) custom-call(f32[16,2,16,2048]{3,2,1,0:T(8,128)S(1)} %get-tuple-element.6.fwd_in, f32[16,2,16,2048]{3,2,1,0:T(8,128)S(1)} %get-tuple-element.7.adj_in, f32[16,2048]{1,0:T(8,128)S(1)} %get-tuple-element.8.grad_in), custom_call_target="tpu_custom_call" | custom-call | tf_op jit(solution)/shard_map/write_out/pallas_call | solution.py:530
where the time goes:
time: 79.9 us; the launch traced here: 79.7 us
  Pallas kernels  77.8 us (97%)
    pallas_call x1, Pallas kernels, local(): pl.pallas_call(functools.partial(step_kernel, count, depth), out_shape=(p...  73.6 us
    pallas_call x1, Pallas kernels, local(): pl.pallas_call(write_kernel, out_shape=(field_shape, field_shape, jax.Sha...  4.19 us

commit v1 on v0

--- a/solution.py
+++ b/solution.py
@@ -13,6 +13,7 @@
 LANES = 128
 QUARTERS = 4
 SUMS = 16
+GROUPS = 2
 VMEM_LIMIT = 50000 * 1024
 
 
@@ -83,16 +84,17 @@
 
 def step_kernel(
     count, depth,
-    turns, wave_k, src_row, mon_row, eps_hbm, field_hbm, adjoint_hbm, mask_hbm, src_hbm, mon_hbm,
+    phase_hbm, wave_hbm, src_row_hbm, mon_row_hbm, eps_hbm, field_hbm, adjoint_hbm, mask_hbm, src_hbm, mon_hbm,
     fwd, adj, grad,
     ext, zed, yed, send, recv, res, img, diag, inverse, eps, eps_send, eps_recv, src, mon, mask,
-    parts, mine, got, coef, gpart, ggot, gtotal, gspread,
+    phase, wave_k, src_row, mon_row, turns, parts, mine, got, coef, gpart, ggot, gtotal, gspread,
     load_sem, side_sem, halo_sems, eps_sems, sum_sems, grad_sems,
 ):
     waves, _, rows, width = field_hbm.shape
     total = rows + TILE
     tiles = width // LANES
     quarter = width // QUARTERS
+    half = waves // GROUPS
     whole = rows * count
     me = lax.axis_index("gx")
     level = lax.axis_index("wa")
@@ -113,27 +115,30 @@
         pltpu.make_async_copy(mon_hbm, mon, side_sem.at[2]),
         pltpu.make_async_copy(mask_hbm, mask, side_sem.at[3]),
     ]
-    sides[0].start()
-    for wave in range(waves):
-        load(0, wave).start()
-    for copy in sides[1:]:
-        copy.start()
-    for wave in range(waves):
-        load(1, wave).start()
-
+    scalars = [
+        pltpu.make_async_copy(phase_hbm, phase, side_sem.at[4]),
+        pltpu.make_async_copy(wave_hbm, wave_k, side_sem.at[5]),
+        pltpu.make_async_copy(src_row_hbm, src_row, side_sem.at[6]),
+        pltpu.make_async_copy(mon_row_hbm, mon_row, side_sem.at[7]),
+    ]
     barrier = pltpu.get_barrier_semaphore()
-    for axis, size, own in (("gx", count, me), ("wa", depth, level)):
+    for axis, size, own in (("wa", depth, level), ("gx", count, me)):
         for hop in range(1, size):
             pl.semaphore_signal(
                 barrier, inc=1, device_id={axis: lax.rem(own + hop, size)},
                 device_id_type=pl.DeviceIdType.MESH,
             )
+    sides[0].start()
+    for wave in range(waves):
+        load(0, wave).start()
+    for copy in scalars + sides[1:]:
+        copy.start()
 
     sides[0].wait()
-    for way, low in ((0, 0), (1, rows - REACH)):
+    for way, low in ((0, 0), (1, rows - 2)):
         for part in range(QUARTERS):
             span = slice(part * quarter, (part + 1) * quarter)
-            eps_send[way, part * 4 : part * 4 + REACH] = eps[low : low + REACH, span]
+            eps_send[way, part * 2 : part * 2 + 2] = eps[low : low + 2, span]
 
     def neighbour(way):
         return {"gx": before if way == 0 else after}
@@ -175,8 +180,15 @@
         return carry
 
     lax.fori_loop(0, waves, first_sends, 0)
-    for copy in sides[1:]:
+    for wave in range(waves):
+        load(1, wave).start()
+    for copy in scalars + sides[1:]:
         copy.wait()
+    wave_of = lax.broadcasted_iota(jnp.int32, (waves, LANES), 0)
+    angle = jnp.zeros((waves, LANES), jnp.float32)
+    for wave in range(waves):
+        angle = jnp.where(wave_of == wave, phase[wave], angle)
+    turns[0], turns[1] = jnp.cos(angle), jnp.sin(angle)
 
     def adjoint_packs(wave, carry):
         load(1, wave).wait()
@@ -185,12 +197,12 @@
 
     lax.fori_loop(0, waves, adjoint_packs, 0)
 
-    for way, at in ((0, rows), (1, total - REACH)):
+    eps[rows:] = jnp.ones((TILE, width), jnp.float32)
+    for way, at in ((0, rows), (1, total - 2)):
         eps_move(way).wait_recv()
         for part in range(QUARTERS):
             span = slice(part * quarter, (part + 1) * quarter)
-            eps[at : at + REACH, span] = eps_recv[way, part * 4 : part * 4 + REACH]
-    eps[rows + REACH : total - REACH] = jnp.ones((TILE - 2 * REACH, width), jnp.float32)
+            eps[at : at + 2, span] = eps_recv[way, part * 2 : part * 2 + 2]
 
     row_of = lax.broadcasted_iota(jnp.int32, (total, LANES), 0)
 
@@ -204,7 +216,7 @@
         return spot
 
     def turn_of(spot, wave, sign):
-        cosine, sine = turns[0, wave], sign * turns[1, wave]
+        cosine, sine = turns[0, pl.ds(wave, 1)], sign * turns[1, pl.ds(wave, 1)]
         above = (spot >= rows) & (spot < rows + REACH) & at_last
         below = (spot >= rows + REACH) & at_first
         turn_c = jnp.where(above | below, cosine, 1.0)
@@ -212,18 +224,17 @@
         return turn_c, turn_s
 
     def unpack(field, wave, sign):
-        cosine, sine = turns[0, wave], sign * turns[1, wave]
+        cosine, sine = turns[0, pl.ds(wave, 1)], sign * turns[1, pl.ds(wave, 1)]
         for way, at in ((0, rows), (1, total - REACH)):
             edge = at_last if way == 0 else at_first
             turn_c = jnp.where(edge, cosine, 1.0)
             turn_s = jnp.where(edge, sine if way == 0 else -sine, 0.0)
-            for part in range(QUARTERS):
-                span = slice(part * quarter, (part + 1) * quarter)
-                base = part * 2 * REACH
-                got_re = recv[field, way, wave, base : base + REACH]
-                got_im = recv[field, way, wave, base + REACH : base + 2 * REACH]
-                ext[field, wave, 0, at : at + REACH, span] = turn_c * got_re - turn_s * got_im
-                ext[field, wave, 1, at : at + REACH, span] = turn_s * got_re + turn_c * got_im
+            for ct in range(tiles):
+                base, place = 2 * REACH * (ct // (tiles // QUARTERS)), col(ct % (tiles // QUARTERS))
+                got_re = recv[field, way, wave, base : base + REACH, place]
+                got_im = recv[field, way, wave, base + REACH : base + 2 * REACH, place]
+                ext[field, wave, 0, at : at + REACH, col(ct)] = turn_c * got_re - turn_s * got_im
+                ext[field, wave, 1, at : at + REACH, col(ct)] = turn_s * got_re + turn_c * got_im
 
     def images(field, wave, spot, side_row, with_overlap):
         squared_k = wave_k[wave]
@@ -304,34 +315,34 @@
 
         return row
 
-    def sum_over_gx(field):
+    def sum_move(field, group, hop, place):
+        return pltpu.make_async_remote_copy(
+            src_ref=mine.at[field, group], dst_ref=got.at[field, group, place],
+            send_sem=sum_sems.at[0, field, group, hop], recv_sem=sum_sems.at[1, field, group, hop],
+            device_id={"gx": lax.rem(me + hop, count)}, device_id_type=pl.DeviceIdType.MESH,
+        )
+
+    def send_sums(field, group):
         used = 15 if field == 0 else 9
-        lane = lax.broadcasted_iota(jnp.int32, (waves, LANES), 1)
-        packed = jnp.zeros((waves, LANES), jnp.float32)
+        lane = lax.broadcasted_iota(jnp.int32, (half, LANES), 1)
+        packed = jnp.zeros((half, LANES), jnp.float32)
+        members = pl.ds(pl.multiple_of(group * half, half), half)
         for i in range(used):
-            packed = jnp.where(lane == i, jnp.sum(parts[i], axis=1, keepdims=True), packed)
-        mine[field] = packed
-
-        def move(hop, place):
-            return pltpu.make_async_remote_copy(
-                src_ref=mine.at[field], dst_ref=got.at[field, place],
-                send_sem=sum_sems.at[0, field, hop], recv_sem=sum_sems.at[1, field, hop],
-                device_id={"gx": lax.rem(me + hop, count)},
-                device_id_type=pl.DeviceIdType.MESH,
-            )
-
+            packed = jnp.where(lane == i, jnp.sum(parts[i, members], axis=1, keepdims=True), packed)
+        mine[field, group] = packed
+        got[field, group, me] = packed
         for hop in range(1, count):
-            move(hop, me).start()
-        got[field, me] = packed
+            sum_move(field, group, hop, me).start()
+
+    def take_sums(field, group):
         for hop in range(1, count):
-            move(hop, lax.rem(me - hop + count, count)).wait_recv()
-        summed = got[field, 0]
+            sum_move(field, group, hop, lax.rem(me - hop + count, count)).wait_recv()
+        summed = got[field, group, 0]
         for place in range(1, count):
-            summed = summed + got[field, place]
+            summed = summed + got[field, group, place]
+        members = pl.ds(pl.multiple_of(group * half, half), half)
         for i, value in enumerate(scalars_of(summed, field == 0)):
-            coef[field, i] = jnp.broadcast_to(value, (waves, LANES))
-        for hop in range(1, count):
-            move(hop, me).wait_send()
+            coef[field, i, members] = jnp.broadcast_to(value, (half, LANES))
 
     def factors(field, wave, *slots):
         return [coef[field, i, pl.ds(wave, 1)] for i in slots]
@@ -345,16 +356,24 @@
 
     def forward_images(wave, carry):
         for way in range(2):
-            halo_move(1, way, wave).start()
-        for way in range(2):
             halo_move(0, way, wave).wait_recv()
         unpack(0, wave, 1.0)
         spot = spot_of(src_row[wave])
         images(0, wave, spot, profile_row(src, wave, turn_of(spot, wave, 1.0), None), True)
         return carry
 
-    lax.fori_loop(0, waves, forward_images, 0)
-    sum_over_gx(0)
+    def adjoint_sends(wave, carry):
+        for way in range(2):
+            halo_move(1, way, wave).start()
+        return carry
+
+    def forward_group(group, carry):
+        lax.fori_loop(group * half, (group + 1) * half, forward_images, 0)
+        send_sums(0, group)
+        lax.fori_loop(group * half, (group + 1) * half, adjoint_sends, 0)
+        return carry
+
+    lax.fori_loop(0, GROUPS, forward_group, 0)
 
     def adjoint_images(wave, carry):
         b, g, over = factors(0, wave, 0, 1), factors(0, wave, 2, 3), factors(0, wave, 4, 5)
@@ -367,17 +386,22 @@
         images(1, wave, spot, profile_row(mon, wave, turn_of(spot, wave, -1.0), over), False)
         return carry
 
-    lax.fori_loop(0, waves, adjoint_images, 0)
-    sum_over_gx(1)
+    def adjoint_group(group, carry):
+        take_sums(0, group)
+        lax.fori_loop(group * half, (group + 1) * half, adjoint_images, 0)
+        send_sums(1, group)
+        return carry
+
+    lax.fori_loop(0, GROUPS, adjoint_group, 0)
 
     piece = width // depth
 
     def columns(place):
         return slice(place * piece, (place + 1) * piece)
 
-    def scatter(hop, to, place):
+    def scatter(hop, place):
         return pltpu.make_async_remote_copy(
-            src_ref=gpart.at[to], dst_ref=ggot.at[place],
+            src_ref=gpart.at[hop], dst_ref=ggot.at[place],
             send_sem=grad_sems.at[0, hop], recv_sem=grad_sems.at[1, hop],
             device_id={"wa": lax.rem(level + hop, depth)}, device_id_type=pl.DeviceIdType.MESH,
         )
@@ -389,33 +413,40 @@
             device_id={"wa": lax.rem(level + hop, depth)}, device_id_type=pl.DeviceIdType.MESH,
         )
 
-    for place in range(depth):
-        def finish(wave, terms):
-            b, g = factors(1, wave, 0, 1), factors(1, wave, 2, 3)
-            scale = 2.0 * wave_k[wave]
-            fresh = []
-            for i in range(piece // LANES):
-                span = col(place * (piece // LANES) + i)
-                out_re, out_im = result(1, wave, b, g, span)
-                adj[wave, 0, :, span] = out_re
-                adj[wave, 1, :, span] = out_im
-                fresh.append(
-                    terms[i] + scale * (out_re * fwd[wave, 0, :, span] - out_im * fwd[wave, 1, :, span])
-                )
-            return tuple(fresh)
-
-        terms = lax.fori_loop(
-            0, waves, finish,
-            tuple(jnp.zeros((rows, LANES), jnp.float32) for _ in range(piece // LANES)),
-        )
-        for i, term in enumerate(terms):
-            gpart[place, :, col(i)] = term
+    hops = [*range(1, depth), 0]
+    for group in range(GROUPS):
+        take_sums(1, group)
+        for hop in hops:
+            base = lax.rem(level + hop, depth) * piece
+            spans = [
+                pl.ds(pl.multiple_of(base + i * LANES, LANES), LANES)
+                for i in range(piece // LANES)
+            ]
+
+            def finish(wave, terms):
+                b, g = factors(1, wave, 0, 1), factors(1, wave, 2, 3)
+                scale = 2.0 * wave_k[wave]
+                fresh = []
+                for span, term in zip(spans, terms):
+                    out_re, out_im = result(1, wave, b, g, span)
+                    adj[wave, 0, :, span] = out_re
+                    adj[wave, 1, :, span] = out_im
+                    fwd_re, fwd_im = fwd[wave, 0, :, span], fwd[wave, 1, :, span]
+                    fresh.append(term + scale * (out_re * fwd_re - out_im * fwd_im))
+                return tuple(fresh)
+
+            zero = jnp.zeros((rows, LANES), jnp.float32)
+            terms = lax.fori_loop(
+                group * half, (group + 1) * half, finish,
+                tuple(gpart[hop, :, col(i)] if group else zero for i in range(piece // LANES)),
+            )
+            for i, term in enumerate(terms):
+                gpart[hop, :, col(i)] = term
+            if group == GROUPS - 1 and hop:
+                scatter(hop, level).start()
+    ggot[level] = gpart[0]
     for hop in range(1, depth):
-        scatter(hop, lax.rem(level + hop, depth), level).start()
-    ggot[level] = gpart[level]
-    for hop in range(1, depth):
-        from_place = lax.rem(level - hop + depth, depth)
-        scatter(hop, from_place, from_place).wait_recv()
+        scatter(hop, lax.rem(level - hop + depth, depth)).wait_recv()
     summed = ggot[0]
     for place in range(1, depth):
         summed = summed + ggot[place]
@@ -428,7 +459,7 @@
     for place in range(depth):
         grad[:, columns(place)] = mask[:, columns(place)].astype(jnp.float32) * gspread[place]
     for hop in range(1, depth):
-        scatter(hop, lax.rem(level + hop, depth), level).wait_send()
+        scatter(hop, level).wait_send()
         gather(hop, level).wait_send()
     for way in range(2):
         eps_move(way).wait_send()
@@ -440,6 +471,10 @@
         return carry
 
     lax.fori_loop(0, waves, drain, 0)
+    for field in range(2):
+        for group in range(GROUPS):
+            for hop in range(1, count):
+                sum_move(field, group, hop, me).wait_send()
 
 
 def write_kernel(fwd_in, adj_in, grad_in, fwd, adj, grad, sems):
@@ -448,9 +483,9 @@
     for wave in range(waves):
         copies.append(pltpu.make_async_copy(fwd_in.at[wave], fwd.at[wave], sems.at[0, wave]))
         copies.append(pltpu.make_async_copy(adj_in.at[wave], adj.at[wave], sems.at[1, wave]))
+    copies.append(pltpu.make_async_copy(grad_in, grad, sems.at[0, waves]))
     for copy in copies:
         copy.start()
-    grad[...] = grad_in[...]
     for copy in copies:
         copy.wait()
 
@@ -470,9 +505,7 @@
     waves, _, rows, width = warm_field.shape
     total = rows + TILE
     count, depth = lax.axis_size("gx"), lax.axis_size("wa")
-    turns = jnp.stack([jnp.cos(bloch_phase), jnp.sin(bloch_phase)])
-
-    smem = pl.BlockSpec(memory_space=pltpu.SMEM)
+
     vmem = pl.BlockSpec(memory_space=pltpu.VMEM)
     anywhere = pl.BlockSpec(memory_space=pl.ANY)
     f32 = jnp.float32
@@ -485,7 +518,7 @@
             pltpu.VMEM(warm_field.shape, f32),
             pltpu.VMEM((rows, width), f32),
         ),
-        in_specs=[smem] * 4 + [anywhere] * 6,
+        in_specs=[anywhere] * 10,
         out_specs=(vmem, vmem, vmem),
         scratch_shapes=[
             pltpu.VMEM((2, waves, 2, total, width), f32),
@@ -498,24 +531,29 @@
             pltpu.VMEM((total, width), f32),
             pltpu.VMEM((total, width), f32),
             pltpu.VMEM((total, width), f32),
-            pltpu.VMEM((2, 4 * QUARTERS, width // QUARTERS), f32),
-            pltpu.VMEM((2, 4 * QUARTERS, width // QUARTERS), f32),
+            pltpu.VMEM((2, 2 * QUARTERS, width // QUARTERS), f32),
+            pltpu.VMEM((2, 2 * QUARTERS, width // QUARTERS), f32),
             pltpu.VMEM(source_profile.shape, f32),
             pltpu.VMEM(monitor_profile.shape, f32),
             pltpu.VMEM((rows, width), jnp.int32),
+            pltpu.SMEM((waves,), f32),
+            pltpu.SMEM((waves,), f32),
+            pltpu.SMEM((waves,), jnp.int32),
+            pltpu.SMEM((waves,), jnp.int32),
+            pltpu.VMEM((2, waves, LANES), f32),
             pltpu.VMEM((SUMS, waves, LANES), f32),
-            pltpu.VMEM((2, waves, LANES), f32),
-            pltpu.VMEM((2, count, waves, LANES), f32),
+            pltpu.VMEM((2, GROUPS, waves // GROUPS, LANES), f32),
+            pltpu.VMEM((2, GROUPS, count, waves // GROUPS, LANES), f32),
             pltpu.VMEM((2, 6, waves, LANES), f32),
             pltpu.VMEM((depth, *piece), f32),
             pltpu.VMEM((depth, *piece), f32),
             pltpu.VMEM(piece, f32),
             pltpu.VMEM((depth, *piece), f32),
             pltpu.SemaphoreType.DMA((2, waves)),
-            pltpu.SemaphoreType.DMA((4,)),
+            pltpu.SemaphoreType.DMA((8,)),
             pltpu.SemaphoreType.DMA((2, 2, 2, waves)),
             pltpu.SemaphoreType.DMA((2, 2)),
-            pltpu.SemaphoreType.DMA((2, 2, count)),
+            pltpu.SemaphoreType.DMA((2, 2, GROUPS, count)),
             pltpu.SemaphoreType.DMA((4, depth)),
         ],
         compiler_params=pltpu.CompilerParams(
@@ -523,7 +561,7 @@
         ),
         name="step",
     )(
-        turns, wavenumber, source_row, monitor_row, permittivity, warm_field, warm_adjoint,
+        bloch_phase, wavenumber, source_row, monitor_row, permittivity, warm_field, warm_adjoint,
         design_mask, source_profile, monitor_profile,
     )
     field_shape = jax.ShapeDtypeStruct(warm_field.shape, f32)
@@ -531,8 +569,8 @@
         write_kernel,
         out_shape=(field_shape, field_shape, jax.ShapeDtypeStruct((rows, width), f32)),
         in_specs=[vmem, vmem, vmem],
-        out_specs=(anywhere, anywhere, vmem),
-        scratch_shapes=[pltpu.SemaphoreType.DMA((2, waves))],
+        out_specs=(anywhere, anywhere, anywhere),
+        scratch_shapes=[pltpu.SemaphoreType.DMA((2, waves + 1))],
         compiler_params=pltpu.CompilerParams(vmem_limit_bytes=1024 * 1024),
         name="write_out",
     )(fwd, adj, grad)

time: 79.9 us -> 62.2 us (0.78)
  Pallas kernels: 77.8 us -> 61.4 us
    pallas_call x1, Pallas kernels: 73.6 us -> 57.8 us  [local(): pl.pallas_call(functools.partial(step_kernel, count, depth), out_shape=(p...]
where the time goes in v1:
time: 62.2 us; the launch traced here: 62.1 us
  Pallas kernels  61.4 us (99%)
  between operations  0.64 us (1%)
    pallas_call x1, Pallas kernels, local(): pl.pallas_call(functools.partial(step_kernel, count, depth), out_shape=(p...  57.8 us
    pallas_call x1, Pallas kernels, local(): pl.pallas_call(write_kernel, out_shape=(field_shape, field_shape, jax.Sha...  3.59 us

profile of v1, /device:TPU:0, one launch (start us, length us, event | category | flops | bytes accessed | tf_op | source)
XLA Modules:
  0.0 62.1 jit_solution(3894600360775293500)
XLA Ops:
  0.6 57.8 %step.1 = (f32[16,2,16,2048]{3,2,1,0:T(8,128)S(1)}, f32[16,2,16,2048]{3,2,1,0:T(8,128)S(1)}, f32[16,2048]{1,0:T(8,128)S(1)}) custom-call(f32[16]{0:T(128)} %phase_hbm.1, f32[16]{0:T(128)} %wave_hbm.1, s32[16]{0:T(128)} %src_row_hbm.1, s32[16]{0:T(128)} %mon_row_hbm.1, f32[16,2048]{1,0:T(8,128)} %eps_hbm.1, f32[16,2,16,2048]{3,2,1,0:T(8,128)} %field_hbm.1, ...), custom_call_target="tpu_custom_call" | custom-call | tf_op jit(solution)/shard_map/step/pallas_call | solution.py:514
  58.5 3.6 %write_out.1 = (f32[16,2,16,2048]{3,2,1,0:T(8,128)}, f32[16,2,16,2048]{3,2,1,0:T(8,128)}, f32[16,2048]{1,0:T(8,128)}) custom-call(f32[16,2,16,2048]{3,2,1,0:T(8,128)S(1)} %get-tuple-element.6.fwd_in, f32[16,2,16,2048]{3,2,1,0:T(8,128)S(1)} %get-tuple-element.7.adj_in, f32[16,2048]{1,0:T(8,128)S(1)} %get-tuple-element.8.grad_in), custom_call_target="tpu_custom_call" | custom-call | tf_op jit(solution)/shard_map/write_out/pallas_call | solution.py:568

commit v2 on v1

--- a/solution.py
+++ b/solution.py
@@ -13,7 +13,7 @@
 LANES = 128
 QUARTERS = 4
 SUMS = 16
-GROUPS = 2
+GROUPS = 4
 VMEM_LIMIT = 50000 * 1024
 
 
@@ -88,13 +88,13 @@
     fwd, adj, grad,
     ext, zed, yed, send, recv, res, img, diag, inverse, eps, eps_send, eps_recv, src, mon, mask,
     phase, wave_k, src_row, mon_row, turns, parts, mine, got, coef, gpart, ggot, gtotal, gspread,
-    load_sem, side_sem, halo_sems, eps_sems, sum_sems, grad_sems,
+    load_sem, side_sem, sent_sem, halo_sem, eps_sems, sum_sems, grad_sems,
 ):
     waves, _, rows, width = field_hbm.shape
     total = rows + TILE
     tiles = width // LANES
     quarter = width // QUARTERS
-    half = waves // GROUPS
+    size = waves // GROUPS
     whole = rows * count
     me = lax.axis_index("gx")
     level = lax.axis_index("wa")
@@ -103,10 +103,11 @@
 
     fields = (field_hbm, adjoint_hbm)
 
-    def load(field, wave):
+    def load(field, group):
+        members = pl.ds(group * size, size)
         return pltpu.make_async_copy(
-            fields[field].at[wave], ext.at[field, wave, :, pl.ds(0, rows)],
-            load_sem.at[field, wave],
+            fields[field].at[members], ext.at[field, members, :, pl.ds(0, rows)],
+            load_sem.at[field, group],
         )
 
     sides = [
@@ -122,15 +123,15 @@
         pltpu.make_async_copy(mon_row_hbm, mon_row, side_sem.at[7]),
     ]
     barrier = pltpu.get_barrier_semaphore()
-    for axis, size, own in (("wa", depth, level), ("gx", count, me)):
-        for hop in range(1, size):
+    for axis, extent, own in (("wa", depth, level), ("gx", count, me)):
+        for hop in range(1, extent):
             pl.semaphore_signal(
-                barrier, inc=1, device_id={axis: lax.rem(own + hop, size)},
+                barrier, inc=1, device_id={axis: lax.rem(own + hop, extent)},
                 device_id_type=pl.DeviceIdType.MESH,
             )
     sides[0].start()
-    for wave in range(waves):
-        load(0, wave).start()
+    for group in range(GROUPS):
+        load(0, group).start()
     for copy in scalars + sides[1:]:
         copy.start()
 
@@ -153,8 +154,14 @@
     def halo_move(field, way, wave):
         return pltpu.make_async_remote_copy(
             src_ref=send.at[field, way, wave], dst_ref=recv.at[field, way, wave],
-            send_sem=halo_sems.at[0, field, way, wave],
-            recv_sem=halo_sems.at[1, field, way, wave],
+            send_sem=sent_sem.at[field, way], recv_sem=halo_sem.at[field, way, wave],
+            device_id=neighbour(way), device_id_type=pl.DeviceIdType.MESH,
+        )
+
+    def halos_sent(field, way):
+        return pltpu.make_async_remote_copy(
+            src_ref=send.at[field, way], dst_ref=recv.at[field, way],
+            send_sem=sent_sem.at[field, way], recv_sem=halo_sem.at[field, way, 0],
             device_id=neighbour(way), device_id_type=pl.DeviceIdType.MESH,
         )
 
@@ -172,16 +179,20 @@
     for way in range(2):
         eps_move(way).start()
 
-    def first_sends(wave, carry):
-        load(0, wave).wait()
-        pack(0, wave)
-        for way in range(2):
-            halo_move(0, way, wave).start()
-        return carry
-
-    lax.fori_loop(0, waves, first_sends, 0)
-    for wave in range(waves):
-        load(1, wave).start()
+    def first_sends(group, carry):
+        load(0, group).wait()
+
+        def each(wave, carry):
+            pack(0, wave)
+            for way in range(2):
+                halo_move(0, way, wave).start()
+            return carry
+
+        return lax.fori_loop(group * size, (group + 1) * size, each, carry)
+
+    lax.fori_loop(0, GROUPS, first_sends, 0)
+    for group in range(GROUPS):
+        load(1, group).start()
     for copy in scalars + sides[1:]:
         copy.wait()
     wave_of = lax.broadcasted_iota(jnp.int32, (waves, LANES), 0)
@@ -190,12 +201,18 @@
         angle = jnp.where(wave_of == wave, phase[wave], angle)
     turns[0], turns[1] = jnp.cos(angle), jnp.sin(angle)
 
-    def adjoint_packs(wave, carry):
-        load(1, wave).wait()
-        pack(1, wave)
-        return carry
-
-    lax.fori_loop(0, waves, adjoint_packs, 0)
+    gpart[...] = jnp.zeros(gpart.shape, jnp.float32)
+
+    def adjoint_packs(group, carry):
+        load(1, group).wait()
+
+        def each(wave, carry):
+            pack(1, wave)
+            return carry
+
+        return lax.fori_loop(group * size, (group + 1) * size, each, carry)
+
+    lax.fori_loop(0, GROUPS, adjoint_packs, 0)
 
     eps[rows:] = jnp.ones((TILE, width), jnp.float32)
     for way, at in ((0, rows), (1, total - 2)):
@@ -236,7 +253,8 @@
                 ext[field, wave, 0, at : at + REACH, col(ct)] = turn_c * got_re - turn_s * got_im
                 ext[field, wave, 1, at : at + REACH, col(ct)] = turn_s * got_re + turn_c * got_im
 
-    def images(field, wave, spot, side_row, with_overlap):
+    def images(field, group, slot, spot, side_row, with_overlap):
+        wave = group * size + slot
         squared_k = wave_k[wave]
         for ct in range(tiles):
             d = 4.0 - squared_k * eps[:, col(ct)]
@@ -280,7 +298,7 @@
             ]
             sums = found if sums is None else [a + b for a, b in zip(sums, found)]
         for i, value in enumerate(sums):
-            parts[i, pl.ds(wave, 1)] = jnp.sum(value, axis=0, keepdims=True)
+            parts[group, i, pl.ds(slot, 1)] = jnp.sum(value, axis=0, keepdims=True)
         if with_overlap:
             away = mon_row[wave] - me * rows
             inside = jnp.where((away >= 0) & (away < rows), 1.0, 0.0)
@@ -300,8 +318,8 @@
                     new_im = m[0] * f[1] - m[1] * f[0]
                     sum_re = new_re if sum_re is None else sum_re + new_re
                     sum_im = new_im if sum_im is None else sum_im + new_im
-                parts[9 + 2 * i, pl.ds(wave, 1)] = inside * sum_re
-                parts[10 + 2 * i, pl.ds(wave, 1)] = inside * sum_im
+                parts[group, 9 + 2 * i, pl.ds(slot, 1)] = inside * sum_re
+                parts[group, 10 + 2 * i, pl.ds(slot, 1)] = inside * sum_im
 
     def profile_row(profile, wave, turn, over):
         turn_c, turn_s = turn
@@ -318,34 +336,47 @@
     def sum_move(field, group, hop, place):
         return pltpu.make_async_remote_copy(
             src_ref=mine.at[field, group], dst_ref=got.at[field, group, place],
-            send_sem=sum_sems.at[0, field, group, hop], recv_sem=sum_sems.at[1, field, group, hop],
+            send_sem=sum_sems.at[0, field, group], recv_sem=sum_sems.at[1, field, group],
             device_id={"gx": lax.rem(me + hop, count)}, device_id_type=pl.DeviceIdType.MESH,
         )
+
+    def all_sums(field, group):
+        others = got.at[field, group, pl.ds(0, count - 1)]
+        return pltpu.make_async_remote_copy(
+            src_ref=others, dst_ref=others,
+            send_sem=sum_sems.at[0, field, group], recv_sem=sum_sems.at[1, field, group],
+            device_id={"gx": after}, device_id_type=pl.DeviceIdType.MESH,
+        )
+
+    slot_of = lax.broadcasted_iota(jnp.int32, (size, LANES), 0)
+    lane_of = lax.broadcasted_iota(jnp.int32, (size, LANES), 1)
 
     def send_sums(field, group):
         used = 15 if field == 0 else 9
-        lane = lax.broadcasted_iota(jnp.int32, (half, LANES), 1)
-        packed = jnp.zeros((half, LANES), jnp.float32)
-        members = pl.ds(pl.multiple_of(group * half, half), half)
+        packed = jnp.zeros((size, LANES), jnp.float32)
         for i in range(used):
-            packed = jnp.where(lane == i, jnp.sum(parts[i, members], axis=1, keepdims=True), packed)
-        mine[field, group] = packed
-        got[field, group, me] = packed
+            own = jnp.sum(parts[group, i], axis=1, keepdims=True)
+            packed = jnp.where(lane_of == slot_of * SUMS + i, own, packed)
+        line = jnp.sum(packed, axis=0, keepdims=True)
+        mine[field, group] = line
+        got[field, group, me] = line
         for hop in range(1, count):
             sum_move(field, group, hop, me).start()
 
     def take_sums(field, group):
-        for hop in range(1, count):
-            sum_move(field, group, hop, lax.rem(me - hop + count, count)).wait_recv()
-        summed = got[field, group, 0]
+        all_sums(field, group).wait_recv()
+        line = got[field, group, 0]
         for place in range(1, count):
-            summed = summed + got[field, group, place]
-        members = pl.ds(pl.multiple_of(group * half, half), half)
+            line = line + got[field, group, place]
+        summed = jnp.broadcast_to(line, (size, LANES))
+        for slot in range(1, size):
+            turned = pltpu.roll(line, LANES - slot * SUMS, 1)
+            summed = jnp.where(slot_of == slot, turned, summed)
         for i, value in enumerate(scalars_of(summed, field == 0)):
-            coef[field, i, members] = jnp.broadcast_to(value, (half, LANES))
-
-    def factors(field, wave, *slots):
-        return [coef[field, i, pl.ds(wave, 1)] for i in slots]
+            coef[field, group, i] = jnp.broadcast_to(value, (size, LANES))
+
+    def factors(field, group, slot, *kinds):
+        return [coef[field, group, i, pl.ds(slot, 1)] for i in kinds]
 
     def result(field, wave, b, g, span):
         x = [ext[field, wave, c, 0:rows, span] for c in range(2)]
@@ -354,41 +385,55 @@
         bz, gy = times(b, z), times(g, y)
         return x[0] + bz[0] + gy[0], x[1] + bz[1] + gy[1]
 
-    def forward_images(wave, carry):
-        for way in range(2):
-            halo_move(0, way, wave).wait_recv()
-        unpack(0, wave, 1.0)
-        spot = spot_of(src_row[wave])
-        images(0, wave, spot, profile_row(src, wave, turn_of(spot, wave, 1.0), None), True)
+    def forward_group(group, carry):
+        def each(slot, carry):
+            wave = group * size + slot
+            for way in range(2):
+                halo_move(0, way, wave).wait_recv()
+            unpack(0, wave, 1.0)
+            spot = spot_of(src_row[wave])
+            side = profile_row(src, wave, turn_of(spot, wave, 1.0), None)
+            images(0, group, slot, spot, side, True)
+            return carry
+
+        lax.fori_loop(0, size, each, 0)
+        send_sums(0, group)
+
+        def adjoint_sends(wave, carry):
+            for way in range(2):
+                halo_move(1, way, wave).start()
+            return carry
+
+        @pl.when(group == GROUPS - 3)
+        def _():
+            lax.fori_loop(0, size, adjoint_sends, 0)
+
+        @pl.when(group == GROUPS - 1)
+        def _():
+            lax.fori_loop(size, waves, adjoint_sends, 0)
+
         return carry
 
-    def adjoint_sends(wave, carry):
-        for way in range(2):
-            halo_move(1, way, wave).start()
-        return carry
-
-    def forward_group(group, carry):
-        lax.fori_loop(group * half, (group + 1) * half, forward_images, 0)
-        send_sums(0, group)
-        lax.fori_loop(group * half, (group + 1) * half, adjoint_sends, 0)
-        return carry
-
     lax.fori_loop(0, GROUPS, forward_group, 0)
-
-    def adjoint_images(wave, carry):
-        b, g, over = factors(0, wave, 0, 1), factors(0, wave, 2, 3), factors(0, wave, 4, 5)
-        for ct in range(tiles):
-            fwd[wave, 0, :, col(ct)], fwd[wave, 1, :, col(ct)] = result(0, wave, b, g, col(ct))
-        for way in range(2):
-            halo_move(1, way, wave).wait_recv()
-        unpack(1, wave, -1.0)
-        spot = spot_of(mon_row[wave])
-        images(1, wave, spot, profile_row(mon, wave, turn_of(spot, wave, -1.0), over), False)
-        return carry
 
     def adjoint_group(group, carry):
         take_sums(0, group)
-        lax.fori_loop(group * half, (group + 1) * half, adjoint_images, 0)
+
+        def each(slot, carry):
+            wave = group * size + slot
+            b, g = factors(0, group, slot, 0, 1), factors(0, group, slot, 2, 3)
+            over = factors(0, group, slot, 4, 5)
+            for ct in range(tiles):
+                fwd[wave, 0, :, col(ct)], fwd[wave, 1, :, col(ct)] = result(0, wave, b, g, col(ct))
+            for way in range(2):
+                halo_move(1, way, wave).wait_recv()
+            unpack(1, wave, -1.0)
+            spot = spot_of(mon_row[wave])
+            side = profile_row(mon, wave, turn_of(spot, wave, -1.0), over)
+            images(1, group, slot, spot, side, False)
+            return carry
+
+        lax.fori_loop(0, size, each, 0)
         send_sums(1, group)
         return carry
 
@@ -402,51 +447,66 @@
     def scatter(hop, place):
         return pltpu.make_async_remote_copy(
             src_ref=gpart.at[hop], dst_ref=ggot.at[place],
-            send_sem=grad_sems.at[0, hop], recv_sem=grad_sems.at[1, hop],
+            send_sem=grad_sems.at[0], recv_sem=grad_sems.at[1],
             device_id={"wa": lax.rem(level + hop, depth)}, device_id_type=pl.DeviceIdType.MESH,
         )
 
     def gather(hop, place):
         return pltpu.make_async_remote_copy(
             src_ref=gtotal, dst_ref=gspread.at[place],
-            send_sem=grad_sems.at[2, hop], recv_sem=grad_sems.at[3, hop],
+            send_sem=grad_sems.at[2], recv_sem=grad_sems.at[3],
             device_id={"wa": lax.rem(level + hop, depth)}, device_id_type=pl.DeviceIdType.MESH,
         )
 
-    hops = [*range(1, depth), 0]
-    for group in range(GROUPS):
+    def all_pieces(held, kind):
+        others = held.at[pl.ds(0, depth - 1)]
+        return pltpu.make_async_remote_copy(
+            src_ref=others, dst_ref=others,
+            send_sem=grad_sems.at[2 * kind], recv_sem=grad_sems.at[2 * kind + 1],
+            device_id={"wa": lax.rem(level + 1, depth)}, device_id_type=pl.DeviceIdType.MESH,
+        )
+
+    def finish(group, hop):
+        base = lax.rem(level + hop, depth) * piece
+        waves_in = []
+        for slot in range(size):
+            wave = group * size + slot
+            b, g = factors(1, group, slot, 0, 1), factors(1, group, slot, 2, 3)
+            waves_in.append((wave, b, g, 2.0 * wave_k[wave]))
+        for i in range(piece // LANES):
+            span = pl.ds(pl.multiple_of(base + i * LANES, LANES), LANES)
+            term = gpart[hop, :, col(i)]
+            for wave, b, g, scale in waves_in:
+                out_re, out_im = result(1, wave, b, g, span)
+                adj[wave, 0, :, span] = out_re
+                adj[wave, 1, :, span] = out_im
+                fwd_re, fwd_im = fwd[wave, 0, :, span], fwd[wave, 1, :, span]
+                term = term + scale * (out_re * fwd_re - out_im * fwd_im)
+            gpart[hop, :, col(i)] = term
+
+    def early_group(group, carry):
         take_sums(1, group)
-        for hop in hops:
-            base = lax.rem(level + hop, depth) * piece
-            spans = [
-                pl.ds(pl.multiple_of(base + i * LANES, LANES), LANES)
-                for i in range(piece // LANES)
-            ]
-
-            def finish(wave, terms):
-                b, g = factors(1, wave, 0, 1), factors(1, wave, 2, 3)
-                scale = 2.0 * wave_k[wave]
-                fresh = []
-                for span, term in zip(spans, terms):
-                    out_re, out_im = result(1, wave, b, g, span)
-                    adj[wave, 0, :, span] = out_re
-                    adj[wave, 1, :, span] = out_im
-                    fwd_re, fwd_im = fwd[wave, 0, :, span], fwd[wave, 1, :, span]
-                    fresh.append(term + scale * (out_re * fwd_re - out_im * fwd_im))
-                return tuple(fresh)
-
-            zero = jnp.zeros((rows, LANES), jnp.float32)
-            terms = lax.fori_loop(
-                group * half, (group + 1) * half, finish,
-                tuple(gpart[hop, :, col(i)] if group else zero for i in range(piece // LANES)),
-            )
-            for i, term in enumerate(terms):
-                gpart[hop, :, col(i)] = term
-            if group == GROUPS - 1 and hop:
-                scatter(hop, level).start()
+        for hop in range(depth):
+            finish(group, hop)
+        return carry
+
+    lax.fori_loop(0, GROUPS - 1, early_group, 0)
+    for way in range(2):
+        eps_move(way).wait_send()
+        for field in range(2):
+            halos_sent(field, way).wait_send()
+    for group in range(GROUPS - 1):
+        for field in range(2):
+            all_sums(field, group).wait_send()
+    all_sums(0, GROUPS - 1).wait_send()
+
+    take_sums(1, GROUPS - 1)
+    for hop in sorted(range(1, depth), key=lambda hop: -min(hop, depth - hop)):
+        finish(GROUPS - 1, hop)
+        scatter(hop, level).start()
+    finish(GROUPS - 1, 0)
     ggot[level] = gpart[0]
-    for hop in range(1, depth):
-        scatter(hop, lax.rem(level - hop + depth, depth)).wait_recv()
+    all_pieces(ggot, 0).wait_recv()
     summed = ggot[0]
     for place in range(1, depth):
         summed = summed + ggot[place]
@@ -454,27 +514,12 @@
     for hop in range(1, depth):
         gather(hop, level).start()
     gspread[level] = summed
-    for hop in range(1, depth):
-        gather(hop, lax.rem(level - hop + depth, depth)).wait_recv()
+    all_sums(1, GROUPS - 1).wait_send()
+    all_pieces(ggot, 0).wait_send()
+    all_pieces(gspread, 1).wait_recv()
     for place in range(depth):
         grad[:, columns(place)] = mask[:, columns(place)].astype(jnp.float32) * gspread[place]
-    for hop in range(1, depth):
-        scatter(hop, level).wait_send()
-        gather(hop, level).wait_send()
-    for way in range(2):
-        eps_move(way).wait_send()
-
-    def drain(wave, carry):
-        for field in range(2):
-            for way in range(2):
-                halo_move(field, way, wave).wait_send()
-        return carry
-
-    lax.fori_loop(0, waves, drain, 0)
-    for field in range(2):
-        for group in range(GROUPS):
-            for hop in range(1, count):
-                sum_move(field, group, hop, me).wait_send()
+    all_pieces(gspread, 1).wait_send()
 
 
 def write_kernel(fwd_in, adj_in, grad_in, fwd, adj, grad, sems):
@@ -510,6 +555,7 @@
     anywhere = pl.BlockSpec(memory_space=pl.ANY)
     f32 = jnp.float32
     piece = (rows, width // depth)
+    size = waves // GROUPS
     block = (2 * REACH * QUARTERS, width // QUARTERS)
     fwd, adj, grad = pl.pallas_call(
         functools.partial(step_kernel, count, depth),
@@ -541,20 +587,21 @@
             pltpu.SMEM((waves,), jnp.int32),
             pltpu.SMEM((waves,), jnp.int32),
             pltpu.VMEM((2, waves, LANES), f32),
-            pltpu.VMEM((SUMS, waves, LANES), f32),
-            pltpu.VMEM((2, GROUPS, waves // GROUPS, LANES), f32),
-            pltpu.VMEM((2, GROUPS, count, waves // GROUPS, LANES), f32),
-            pltpu.VMEM((2, 6, waves, LANES), f32),
+            pltpu.VMEM((GROUPS, SUMS, size, LANES), f32),
+            pltpu.VMEM((2, GROUPS, 1, LANES), f32),
+            pltpu.VMEM((2, GROUPS, count, 1, LANES), f32),
+            pltpu.VMEM((2, GROUPS, 6, size, LANES), f32),
             pltpu.VMEM((depth, *piece), f32),
             pltpu.VMEM((depth, *piece), f32),
             pltpu.VMEM(piece, f32),
             pltpu.VMEM((depth, *piece), f32),
-            pltpu.SemaphoreType.DMA((2, waves)),
+            pltpu.SemaphoreType.DMA((2, GROUPS)),
             pltpu.SemaphoreType.DMA((8,)),
-            pltpu.SemaphoreType.DMA((2, 2, 2, waves)),
             pltpu.SemaphoreType.DMA((2, 2)),
-            pltpu.SemaphoreType.DMA((2, 2, GROUPS, count)),
-            pltpu.SemaphoreType.DMA((4, depth)),
+            pltpu.SemaphoreType.DMA((2, 2, waves)),
+            pltpu.SemaphoreType.DMA((2, 2)),
+            pltpu.SemaphoreType.DMA((2, 2, GROUPS)),
+            pltpu.SemaphoreType.DMA((4,)),
         ],
         compiler_params=pltpu.CompilerParams(
             collective_id=0, has_side_effects=True, vmem_limit_bytes=VMEM_LIMIT

time: 62.2 us -> 60.3 us (0.969)
  Pallas kernels: 61.4 us -> 59.6 us
    pallas_call x1, Pallas kernels: 57.8 us -> 56 us  [local(): pl.pallas_call(functools.partial(step_kernel, count, depth), out_shape=(p...]
where the time goes in v2:
time: 60.3 us; the launch traced here: 60.2 us
  Pallas kernels  59.6 us (99%)
  between operations  0.64 us (1%)
    pallas_call x1, Pallas kernels, local(): pl.pallas_call(functools.partial(step_kernel, count, depth), out_shape=(p...  56 us
    pallas_call x1, Pallas kernels, local(): pl.pallas_call(write_kernel, out_shape=(field_shape, field_shape, jax.Sha...  3.59 us

profile of v2, /device:TPU:0, one launch (start us, length us, event | category | flops | bytes accessed | tf_op | source)
XLA Modules:
  0.0 60.2 jit_solution(2733408788544075960)
XLA Ops:
  0.6 56.0 %step.1 = (f32[16,2,16,2048]{3,2,1,0:T(8,128)S(1)}, f32[16,2,16,2048]{3,2,1,0:T(8,128)S(1)}, f32[16,2048]{1,0:T(8,128)S(1)}) custom-call(f32[16]{0:T(128)} %phase_hbm.1, f32[16]{0:T(128)} %wave_hbm.1, s32[16]{0:T(128)} %src_row_hbm.1, s32[16]{0:T(128)} %mon_row_hbm.1, f32[16,2048]{1,0:T(8,128)} %eps_hbm.1, f32[16,2,16,2048]{3,2,1,0:T(8,128)} %field_hbm.1, ...), custom_call_target="tpu_custom_call" | custom-call | tf_op jit(solution)/shard_map/step/pallas_call | solution.py:560
  56.6 3.6 %write_out.1 = (f32[16,2,16,2048]{3,2,1,0:T(8,128)}, f32[16,2,16,2048]{3,2,1,0:T(8,128)}, f32[16,2048]{1,0:T(8,128)}) custom-call(f32[16,2,16,2048]{3,2,1,0:T(8,128)S(1)} %get-tuple-element.6.fwd_in, f32[16,2,16,2048]{3,2,1,0:T(8,128)S(1)} %get-tuple-element.7.adj_in, f32[16,2048]{1,0:T(8,128)S(1)} %get-tuple-element.8.grad_in), custom_call_target="tpu_custom_call" | custom-call | tf_op jit(solution)/shard_map/write_out/pallas_call | solution.py:615

commit v3 on v2

--- a/solution.py
+++ b/solution.py
@@ -363,8 +363,7 @@
         for hop in range(1, count):
             sum_move(field, group, hop, me).start()
 
-    def take_sums(field, group):
-        all_sums(field, group).wait_recv()
+    def step_factors(field, group):
         line = got[field, group, 0]
         for place in range(1, count):
             line = line + got[field, group, place]
@@ -374,6 +373,10 @@
             summed = jnp.where(slot_of == slot, turned, summed)
         for i, value in enumerate(scalars_of(summed, field == 0)):
             coef[field, group, i] = jnp.broadcast_to(value, (size, LANES))
+
+    def take_sums(field, group):
+        all_sums(field, group).wait_recv()
+        step_factors(field, group)
 
     def factors(field, group, slot, *kinds):
         return [coef[field, group, i, pl.ds(slot, 1)] for i in kinds]
@@ -485,11 +488,14 @@
             gpart[hop, :, col(i)] = term
 
     def early_group(group, carry):
-        take_sums(1, group)
         for hop in range(depth):
             finish(group, hop)
         return carry
 
+    for group in range(GROUPS - 1):
+        all_sums(1, group).wait_recv()
+    for group in range(GROUPS - 1):
+        step_factors(1, group)
     lax.fori_loop(0, GROUPS - 1, early_group, 0)
     for way in range(2):
         eps_move(way).wait_send()

time: 60.3 us -> 59.9 us (level)
  no operation moved by 1% of the time
where the time goes in v3:
time: 59.9 us; the launch traced here: 59.8 us
  Pallas kernels  59.1 us (99%)
  between operations  0.64 us (1%)
    pallas_call x1, Pallas kernels, local(): pl.pallas_call(functools.partial(step_kernel, count, depth), out_shape=(p...  55.6 us
    pallas_call x1, Pallas kernels, local(): pl.pallas_call(write_kernel, out_shape=(field_shape, field_shape, jax.Sha...  3.59 us

profile of v3, /device:TPU:0, one launch (start us, length us, event | category | flops | bytes accessed | tf_op | source)
XLA Modules:
  0.0 59.8 jit_solution(905950512725975420)
XLA Ops:
  0.6 55.6 %step.1 = (f32[16,2,16,2048]{3,2,1,0:T(8,128)S(1)}, f32[16,2,16,2048]{3,2,1,0:T(8,128)S(1)}, f32[16,2048]{1,0:T(8,128)S(1)}) custom-call(f32[16]{0:T(128)} %phase_hbm.1, f32[16]{0:T(128)} %wave_hbm.1, s32[16]{0:T(128)} %src_row_hbm.1, s32[16]{0:T(128)} %mon_row_hbm.1, f32[16,2048]{1,0:T(8,128)} %eps_hbm.1, f32[16,2,16,2048]{3,2,1,0:T(8,128)} %field_hbm.1, ...), custom_call_target="tpu_custom_call" | custom-call | tf_op jit(solution)/shard_map/step/pallas_call | solution.py:566
  56.2 3.6 %write_out.1 = (f32[16,2,16,2048]{3,2,1,0:T(8,128)}, f32[16,2,16,2048]{3,2,1,0:T(8,128)}, f32[16,2048]{1,0:T(8,128)}) custom-call(f32[16,2,16,2048]{3,2,1,0:T(8,128)S(1)} %get-tuple-element.6.fwd_in, f32[16,2,16,2048]{3,2,1,0:T(8,128)S(1)} %get-tuple-element.7.adj_in, f32[16,2048]{1,0:T(8,128)S(1)} %get-tuple-element.8.grad_in), custom_call_target="tpu_custom_call" | custom-call | tf_op jit(solution)/shard_map/write_out/pallas_call | solution.py:621
